TPU v7x, 128 devices: a whole 4x4x4 slice. The times are simulated.
128 devices in a mesh: tables: 1, g: 128 (over z, y, x, core).
Axes of the slice: x: 4, y: 4, z: 4, core: 2. Of those that a mesh axis runs over, the one named last changes fastest.
Arguments:
- item_factors: float32 [262144, 64], P(('tables', 'g'))
- user_start: float32 [65536, 64], P(('tables', 'g'))
- by_item_idx: int32 [128, 65536, 8], P(('tables', 'g'))
- by_item_conf: float32 [128, 65536, 8], P(('tables', 'g'))
- by_user_idx: int32 [128, 262144, 2], P(('tables', 'g'))
- by_user_conf: float32 [128, 262144, 2], P(('tables', 'g'))
Outputs:
- output 1: float32 [65536, 64], P(('tables', 'g'))
- output 2: float32 [262144, 64], P(('tables', 'g'))
All inputs are finite; a program needn't handle non-finite values.
Results may differ from a plain program's by a relative error of at most 0.0123.
Values are sent between devices in bfloat16 or wider.
A program may use at most 1 GiB of HBM per device.

v0:
```python
import functools

import jax
import jax.numpy as jnp
from jax import lax
from jax.experimental import pallas as pl
from jax.experimental.pallas import tpu as pltpu
from jax.sharding import PartitionSpec as P


REG_LAMBDA = 0.01
CG_STEPS = 3
F = 64
FX = F + 16
PITCH = F + 8
LN = 128
G = 128
PAY = 48
EMPTY = 2048
PACK = 4096
F32 = jnp.float32
BF16 = jnp.bfloat16
I16 = jnp.int16
I32 = jnp.int32


def iota(shape, dim, dtype=I32):
    return lax.broadcasted_iota(dtype, shape, dim)


def take(x, ind, axis):
    other = 1 - axis
    dims = lax.GatherDimensionNumbers(
        offset_dims=(), collapsed_slice_dims=(axis,), start_index_map=(axis,),
        operand_batching_dims=(other,), start_indices_batching_dims=(other,))
    return lax.gather(x, ind[..., None], dims, slice_sizes=(1, 1),
                      mode=lax.GatherScatterMode.PROMISE_IN_BOUNDS)


def dot_nt(a, b):
    return lax.dot_general(a, b, (((1,), (1,)), ((), ())), preferred_element_type=F32)


def fold(gram):
    return jnp.concatenate([gram[:F // 2], gram[F // 2:]], axis=1)


def unfold(gram):
    return jnp.concatenate([gram[:, :F], gram[:, F:]], axis=0)


def table_kernel(x_ref, tab_ref, gram_ref):
    x = x_ref[...].astype(BF16)
    for h in range(x.shape[1] // LN):
        tab_ref[h] = x[:, h * LN:(h + 1) * LN]
    gram_ref[...] = fold(dot_nt(x, x))


def make_table(x_t):
    n = x_t.shape[1]
    return pl.pallas_call(
        table_kernel,
        out_shape=(jax.ShapeDtypeStruct((n // LN, F, LN), BF16), jax.ShapeDtypeStruct((F // 2, LN), F32)),
        name='table',
    )(x_t)


def code_weight(idx, conf):
    code = jnp.where(conf > 0.0, idx, EMPTY).astype(F32)
    return code, jnp.maximum(conf - 1.0, 0.0)


def user_payload_kernel(me_ref, idx_ref, conf_ref, out_ref):
    skew = me_ref[0] % 16
    row, lane = iota((8, LN), 0), iota((8, LN), 1)
    first = (lane - 16 * row) & 127
    second = ((lane >> 4) - row) & 7
    third = ((lane ^ skew) + 16 * row) & 127

    def arrange(x):
        return take(take(take(x, first, 1), second, 0), third, 1)

    def place(dest, _):
        codes = []
        for q in range(4):
            cols = pl.ds(pl.multiple_of(dest * 512 + q * LN, LN), LN)
            code, weight = code_weight(idx_ref[:, cols], conf_ref[:, cols])
            out_ref[dest, pl.ds(q * 8, 8), :] = arrange(weight)
            codes.append(arrange(code))
        for q in range(2):
            out_ref[dest, pl.ds(32 + q * 8, 8), :] = codes[q] + PACK * codes[q + 2]
        return 0

    lax.fori_loop(0, out_ref.shape[0], place, 0, unroll=min(8, out_ref.shape[0]))


def user_payload(me, idx_t, conf_t, dests):
    step = min(32, dests)
    spec = pl.BlockSpec((8, step * 512), lambda i: (0, i))
    return pl.pallas_call(
        user_payload_kernel,
        grid=(dests // step,),
        in_specs=[pl.BlockSpec(memory_space=pltpu.SMEM), spec, spec],
        out_specs=pl.BlockSpec((step, PAY, LN), lambda i: (i, 0, 0)),
        out_shape=jax.ShapeDtypeStruct((dests, PAY, LN), F32),
        name='user_payload',
    )(me, idx_t, conf_t)


def item_payload_kernel(me_ref, idx_ref, conf_ref, out_ref):
    skew = me_ref[0] % 64
    lane = iota((8, LN), 1)
    pattern = lane ^ skew
    low = lane < 64

    def halves(x0, x1):
        a = jnp.where(low, x0, pltpu.roll(x1, 64, 1))
        b = jnp.where(low, pltpu.roll(x0, 64, 1), x1)
        return take(a, pattern, 1), take(b, pattern, 1)

    def place(dest, _):
        for q in range(2):
            base = dest * 32 + q * 16
            rows = [pl.ds(base + j, 8, stride=2) for j in range(2)]
            pairs = [code_weight(idx_ref[r, :], conf_ref[r, :]) for r in rows]
            code_a, code_b = halves(pairs[0][0], pairs[1][0])
            weight_a, weight_b = halves(pairs[0][1], pairs[1][1])
            out_ref[dest, pl.ds(q * 8, 8), :] = weight_a
            out_ref[dest, pl.ds(16 + q * 8, 8), :] = weight_b
            out_ref[dest, pl.ds(32 + q * 8, 8), :] = code_a + PACK * code_b
        return 0

    lax.fori_loop(0, out_ref.shape[0], place, 0, unroll=min(8, out_ref.shape[0]))


def item_payload(me, idx_rows, conf_rows, dests):
    step = min(32, dests)
    spec = pl.BlockSpec((step * 32, LN), lambda i: (i, 0))
    return pl.pallas_call(
        item_payload_kernel,
        grid=(dests // step,),
        in_specs=[pl.BlockSpec(memory_space=pltpu.SMEM), spec, spec],
        out_specs=pl.BlockSpec((step, PAY, LN), lambda i: (i, 0, 0)),
        out_shape=jax.ShapeDtypeStruct((dests, PAY, LN), F32),
        name='item_payload',
    )(me, idx_rows, conf_rows)


ORDERS = ((2, 1, 0), (1, 0, 2), (0, 2, 1))
STRIDES = (32, 8, 2)
RING = 4


def gather_kernel(streams, *refs):
    arrays = len({s[0] for s in streams})
    ins, outs = refs[:arrays], refs[arrays:2 * arrays]
    send, recv, pass_send, pass_recv, local = refs[2 * arrays:]
    me = lax.axis_index('g')
    core = me % 2
    here = [me // stride % RING for stride in STRIDES]
    partner = me + 1 - 2 * core

    def beside(dim, delta):
        return me + ((here[dim] + delta + RING) % RING - here[dim]) * STRIDES[dim]

    barrier = pltpu.get_barrier_semaphore()
    peers = [beside(dim, delta) for dim in range(3) for delta in (1, -1)] + [partner]
    for peer in peers:
        pl.semaphore_signal(barrier, inc=1, device_id={'g': peer}, device_id_type=pl.DeviceIdType.MESH)
    pl.semaphore_wait(barrier, len(peers))

    def region(s, phase, dim, delta, half):
        which, first, rows = streams[s][:3]
        order = ORDERS[streams[s][3]]
        index = []
        for d in range(3):
            if d in order[:phase]:
                index.append(pl.ds(0, RING))
            else:
                index.append((here[d] + delta + RING) % RING if d == dim else here[d])
        if half is not None:
            rows = rows // 2
            first = first + half * rows
        return outs[which].at[(*index, core, pl.ds(first, rows), slice(None))]

    def remote(src, dst, sems, index, peer):
        return pltpu.make_async_remote_copy(
            src_ref=src, dst_ref=dst, send_sem=sems[0].at[index], recv_sem=sems[1].at[index],
            device_id={'g': peer}, device_id_type=pl.DeviceIdType.MESH)

    passed = []

    def pass_on(src, dst, s, slot):
        copy = remote(src, dst, (pass_send, pass_recv), 13 * s + slot, partner)
        copy.start()
        passed.append(copy)

    own, kept = [], []
    for s, (which, first, rows, _) in enumerate(streams):
        src = ins[which].at[pl.ds(first, rows), :]
        own.append(src)
        copy = pltpu.make_async_copy(src, region(s, 0, 0, 0, None), local.at[s])
        copy.start()
        kept.append(copy)
    sent = []
    for phase in range(3):
        across = {}
        for s in range(len(streams)):
            dim = ORDERS[streams[s][3]][phase]
            for way, delta in enumerate((1, -1)):
                mine = region(s, phase, dim, 0, None)
                src = own[s] if phase == 0 else mine
                across[s, way] = remote(src, mine, (send, recv), ((s * 3 + phase) * 2 + 0) * 2 + way, beside(dim, delta))
                across[s, way].start()
        if phase == 0:
            for s in range(len(streams)):
                pass_on(own[s], region(s, 0, 0, 0, None), s, 0)
        further = {}
        for s in range(len(streams)):
            dim = ORDERS[streams[s][3]][phase]
            for way, delta in enumerate((1, -1)):
                across[s, way].wait_recv()
                half = region(s, phase, dim, -delta, way)
                further[s, way] = remote(half, half, (send, recv), ((s * 3 + phase) * 2 + 1) * 2 + way, beside(dim, delta))
                further[s, way].start()
                whole = region(s, phase, dim, -delta, None)
                pass_on(whole, whole, s, 1 + 4 * phase + way)
        for s in range(len(streams)):
            dim = ORDERS[streams[s][3]][phase]
            for way in range(2):
                further[s, way].wait_recv()
                half = region(s, phase, dim, 2, way)
                pass_on(half, half, s, 3 + 4 * phase + way)
        if phase == 0:
            for copy in kept:
                copy.wait()
        sent += list(across.values()) + list(further.values())
    for copy in sent:
        copy.wait_send()
    for copy in passed:
        copy.wait_send()
    for copy in passed:
        copy.wait_recv()


def gather_all(table, gram, collective_id):
    rows = table.shape[0]
    third = rows // 3 // 32 * 32
    sizes = (rows - 2 * third, third, third)
    streams, first = [], 0
    for n, size in enumerate(sizes):
        streams.append((0, first, size, n))
        first += size
    streams.append((1, 0, gram.shape[0], 0))
    count = len(streams)
    any_spec = pl.BlockSpec(memory_space=pl.ANY)
    tables, grams = pl.pallas_call(
        functools.partial(gather_kernel, tuple(streams)),
        in_specs=[pl.BlockSpec(memory_space=pltpu.VMEM)] * 2,
        out_specs=[any_spec] * 2,
        out_shape=[jax.ShapeDtypeStruct((RING, RING, RING, 2, *x.shape), x.dtype) for x in (table, gram)],
        scratch_shapes=[pltpu.SemaphoreType.DMA((12 * count,)), pltpu.SemaphoreType.DMA((12 * count,)),
                        pltpu.SemaphoreType.DMA((13 * count,)), pltpu.SemaphoreType.DMA((13 * count,)),
                        pltpu.SemaphoreType.DMA((count,))],
        compiler_params=pltpu.CompilerParams(collective_id=collective_id, has_side_effects=True),
        name='gather_all',
    )(table, gram)
    return tables.reshape(G, rows, LN), grams.reshape(-1, LN)


def half_kernel(slots, blocks, pair, lanes_of, emit, tab_hbm, pay_hbm, gram_ref, x0_ref, *refs):
    if emit:
        out_ref, tab_ref, gout_ref = refs[:3]
        refs = refs[3:]
    else:
        out_ref = refs[0]
        refs = refs[1:]
    tab, pay, ids, yg, yu_a, yu_b, wu_a, wu_b, a_scr, at_scr, p_scr, s_scr, sems = refs
    per = LN // slots
    chunks = G // per
    groups = LN // per
    steps = blocks * groups // pair
    turns = groups // pair
    heads = tab.shape[1]

    pay_copy = pltpu.make_async_copy(pay_hbm, pay, sems.at[8])
    pay_copy.start()

    def tab_copy(i):
        return pltpu.make_async_copy(tab_hbm.at[pl.ds(16 * i, 16)], tab.at[pl.ds(16 * i, 16)], sems.at[i])

    for i in range(8):
        tab_copy(i).start()
    ids[...] = iota((2 * LN, LN), 0, I16)
    pay_copy.wait()

    lane16 = iota((16, LN), 1, I16)
    lane = iota((8, LN), 1)
    row = iota((8, LN), 0)

    def add_gram(d, acc):
        return acc + gram_ref[pl.ds(pl.multiple_of(d * (F // 2), F // 2), F // 2), :]

    gram = lax.fori_loop(0, G, add_gram, jnp.zeros((F // 2, LN), F32), unroll=8)
    gpad = jnp.concatenate([unfold(gram), jnp.zeros((16, F), F32)], axis=0)
    gpad = jnp.concatenate([gpad, jnp.zeros((FX, 16), F32)], axis=1)
    rr, cc = iota((FX, FX), 0), iota((FX, FX), 1)
    gpad = gpad + jnp.where((rr == cc) & (rr < F), REG_LAMBDA, 0.0)

    def pay_row(t):
        if slots == 8:
            return t, 32 + t % 16, 12 * (t // 16)
        return (t % 2) * 16 + t // 2, 32 + t // 2, 12 * (t % 2)

    def spread_weights(t, wu, q):
        wrow = pay_row(t)[0]
        for c in range(chunks):
            tiles = []
            for v in range(per // 8):
                start = (per * c + 8 * v) * PAY + wrow
                tiles.append(pay[pl.ds(start, 8, stride=PAY), :])
            for bit in (1, 2, 4):
                hit = (lane & bit) != 0
                up = (row & bit) != 0
                for v in range(len(tiles)):
                    x = tiles[v]
                    if bit == 4:
                        other = pltpu.roll(x, 4, 0)
                    else:
                        other = jnp.where(up, pltpu.roll(x, bit, 0), pltpu.roll(x, 8 - bit, 0))
                    tiles[v] = jnp.where(hit, other, x)
            bit = 8
            while bit < per:
                hit = (lane & bit) != 0
                tiles = [jnp.where(hit, tiles[v ^ (bit // 8)], tiles[v]) for v in range(len(tiles))]
                bit *= 2
            for v in range(len(tiles)):
                wu[c, pl.ds(per * q + 8 * v, 8), :] = tiles[v]

    def exchange(xs, low_bit):
        bit, n = 1, len(xs)
        while bit < n:
            hit = (lane16 & I16(bit * low_bit)) != I16(0)
            xs = [jnp.where(hit, xs[a ^ bit], xs[a]) for a in range(n)]
            bit *= 2
        return xs

    def regroup(i, yu):
        for q in range(pair):
            for k in range(4):
                rows = pl.ds(16 * k, 16)
                xs = exchange([yg[q, d, rows, :] for d in range(16)], 1)
                for a in range(16):
                    if slots == 8:
                        yu[16 * q + a, i, rows, :] = xs[a]
                    else:
                        yu[64 * q + (i % 4) * 16 + a, i // 4, rows, :] = xs[a]

    ones = jnp.ones((16, LN * chunks), BF16)

    def form(y_parts, wu, u, at):
        vs = []
        for c in range(chunks):
            w = wu[c, pl.ds(u, 1), :]
            vs.append((y_parts[c].astype(F32) * w).astype(BF16))
        y = jnp.concatenate([jnp.concatenate(y_parts, axis=1), ones], axis=0)
        v = jnp.concatenate([jnp.concatenate(vs, axis=1), ones], axis=0)
        a_scr[pl.ds(at * PITCH, PITCH), pl.ds(0, FX)] = (dot_nt(y, v) + gpad)[:PITCH]

    def form_rows(t, i, yu, wu):
        done = jnp.maximum(t - 1, 0)
        first = done // turns % 2 * LN + done % turns * (per * pair)
        if slots == 8:
            for e in range(2 * pair):
                u = 2 * pair * i + e
                form([yu[u, c] for c in range(chunks)], wu, u, first + u)
        else:
            for q in range(pair):
                for e in range(2):
                    r = 64 * q + 2 * i + e
                    parts = []
                    for c in range(chunks):
                        by_k = [exchange([yu[r + 16 * m, c, pl.ds(16 * k, 16), :] for m in range(4)], 16)
                                for k in range(4)]
                        parts.append([jnp.concatenate([by_k[k][m] for k in range(4)], axis=0) for m in range(4)])
                    for m in range(4):
                        form([parts[c][m] for c in range(chunks)], wu, r + 16 * m, first + r + 16 * m)

    def codes(t, d, q):
        _, crow, shift = pay_row(pair * t + q)
        packed = pay[pl.ds(d * PAY + crow, 1), :].astype(I32)
        return (packed >> shift) & (PACK - 1)

    def by_lanes(t, d, dd, q):
        code = jnp.broadcast_to(codes(t, d, q), (F, LN)).astype(I16)
        low = code & I16(LN - 1)
        head = code >> I16(7)
        acc = jnp.zeros((F, LN), BF16)
        for h in range(heads):
            acc = jnp.where(head == I16(h), take(tab[d, h], low, 1), acc)
        yg[q, dd] = acc

    def by_matmul(t, d, dd):
        hots, halves = [], []
        for q in range(2):
            code = codes(t, d, q)
            low = (jnp.broadcast_to(code, (2 * LN, LN)) & (2 * LN - 1)).astype(I16)
            hots.append(jnp.where(low == ids[...], jnp.ones((2 * LN, LN), BF16), jnp.zeros((2 * LN, LN), BF16)))
            halves.append(jnp.broadcast_to(code, (F, LN)) >> 8)
        table = jnp.concatenate([jnp.concatenate([tab[d, 2 * h], tab[d, 2 * h + 1]], axis=1)
                                 for h in range(heads // 2)], axis=0)
        found = jnp.dot(table, jnp.concatenate(hots, axis=1), preferred_element_type=F32)
        for q in range(2):
            acc = jnp.zeros((F, LN), F32)
            for h in range(heads // 2):
                acc = jnp.where(halves[q] == h, found[h * F:(h + 1) * F, q * LN:(q + 1) * LN], acc)
            yg[q, dd] = acc.astype(BF16)

    def lookup(t, i):
        turn = 0
        for dd in range(16):
            d = 16 * i + dd
            turn += lanes_of
            if turn >= 16:
                turn -= 16
                for q in range(pair):
                    by_lanes(t, d, dd, q)
            else:
                by_matmul(t, d, dd)

    def flip(block, b):
        m = a_scr[pl.ds(block % 2 * (LN * PITCH) + b, LN, stride=PITCH), :].T
        at_scr[b] = m[:F]
        s_scr[pl.ds(b, 1), :] = m[F:F + 1]

    def flip_all(block):
        def four(b4, _):
            for e in range(4):
                flip(block, 4 * b4 + e)
            return 0

        lax.fori_loop(0, F // 4, four, 0)

    def solve(block):
        rhs = a_scr[pl.ds(block % 2 * (LN * PITCH) + F, LN, stride=PITCH), :].T[:F] + s_scr[...]
        x = x0_ref[:, pl.ds(pl.multiple_of(block * LN, LN), LN)]

        def apply_mat(vec):
            p_scr[...] = vec

            def add(b, acc):
                return acc + at_scr[b] * p_scr[pl.ds(b, 1), :]

            return lax.fori_loop(0, F, add, jnp.zeros((F, LN), F32), unroll=8)

        res = rhs - apply_mat(x)
        direction = res
        res_sq = jnp.sum(res * res, axis=0, keepdims=True)
        for step in range(CG_STEPS):
            q = apply_mat(direction)
            length = res_sq / jnp.sum(direction * q, axis=0, keepdims=True)
            x = x + length * direction
            if step + 1 < CG_STEPS:
                res = res - length * q
                new_sq = jnp.sum(res * res, axis=0, keepdims=True)
                direction = res + (new_sq / res_sq) * direction
                res_sq = new_sq
        out_ref[:, pl.ds(pl.multiple_of(block * LN, LN), LN)] = x
        if emit:
            xb = x.astype(BF16)
            tab_ref[block] = xb
            gout_ref[...] += fold(dot_nt(xb, xb))

    if emit:
        gout_ref[...] = jnp.zeros((F // 2, LN), F32)

    def step_pass(t, parts, yu, wu, yu_last, wu_last):
        now = jnp.minimum(t, steps - 1)
        done = jnp.maximum(t - 1, 0)
        before = jnp.maximum(done // turns - 1, 0)
        for q in range(pair):
            spread_weights(pair * now + q, wu, q)

        def inner(i, _):
            @pl.when(t == 0)
            def _():
                tab_copy(i).wait()

            flips = F // (8 * turns)
            for e in range(flips):
                flip(before, (done % turns * 8 + i) * flips + e)
            form_rows(t, i, yu_last, wu_last)
            regroup((i + 7) % 8, yu)
            lookup(now, i)
            return 0

        lax.fori_loop(0, parts, inner, 0)
        regroup(7, yu)

        @pl.when((t >= turns + 1) & (t <= steps) & (t % turns == 0))
        def _():
            solve(t // turns - 2)

    def two_steps(t2, _):
        step_pass(2 * t2, 8, yu_a, wu_a, yu_b, wu_b)
        step_pass(2 * t2 + 1, jnp.where(2 * t2 + 1 <= steps, 8, 0), yu_b, wu_b, yu_a, wu_a)
        return 0

    lax.fori_loop(0, steps // 2 + 1, two_steps, 0)
    flip_all(blocks - 1)
    solve(blocks - 1)


def half_step(slots, emit, pair, lanes_of, tables, payload, gram, x0_t):
    n = x0_t.shape[1]
    heads = tables.shape[1]
    per = LN // slots
    chunks = G // per
    out_shape = [jax.ShapeDtypeStruct((F, n), F32)]
    if emit:
        out_shape += [jax.ShapeDtypeStruct((n // LN, F, LN), BF16), jax.ShapeDtypeStruct((F // 2, LN), F32)]
    vmem = pl.BlockSpec(memory_space=pltpu.VMEM)
    return pl.pallas_call(
        functools.partial(half_kernel, slots, n // LN, pair, lanes_of, emit),
        in_specs=[pl.BlockSpec(memory_space=pl.ANY), pl.BlockSpec(memory_space=pl.ANY), vmem, vmem],
        out_specs=[vmem] * len(out_shape),
        out_shape=out_shape,
        scratch_shapes=[
            pltpu.VMEM((G, heads, F, LN), BF16),
            pltpu.VMEM((G * PAY, LN), F32),
            pltpu.VMEM((2 * LN, LN), I16),
            pltpu.VMEM((pair, 16, F, LN), BF16),
            pltpu.VMEM((pair * per, chunks, F, LN), BF16),
            pltpu.VMEM((pair * per, chunks, F, LN), BF16),
            pltpu.VMEM((chunks, pair * per, LN), F32),
            pltpu.VMEM((chunks, pair * per, LN), F32),
            pltpu.VMEM((2 * LN * PITCH, LN), F32),
            pltpu.VMEM((F, F, LN), F32),
            pltpu.VMEM((F, LN), F32),
            pltpu.VMEM((F, LN), F32),
            pltpu.SemaphoreType.DMA((9,)),
        ],
        compiler_params=pltpu.CompilerParams(vmem_limit_bytes=62 * 1024 * 1024),
        cost_estimate=pl.CostEstimate(flops=10 ** 11, bytes_accessed=2 ** 25, transcendentals=0),
        name='half_step',
    )(tables, payload, gram, x0_t)


def solution(mesh):
    part_spec = P(('tables', 'g'), None)
    slot_spec = P(('tables', 'g'), None, None)

    def local_sweep(item_block, start_block, item_idx, item_conf, user_idx, user_conf):
        me = lax.axis_index('g').astype(I32).reshape(1)
        item_t = item_block.T
        table, gram_part = make_table(item_t)
        payload = user_payload(me, item_idx[0].T, item_conf[0].T, G)
        payload = lax.all_to_all(payload, 'g', 0, 0, tiled=True)

        def as_rows(x):
            return x[0].reshape(-1, LN, 2).transpose(0, 2, 1).reshape(-1, LN)

        late = item_payload(me, as_rows(user_idx), as_rows(user_conf), G)
        late = lax.all_to_all(late, 'g', 0, 0, tiled=True)

        tables, gram_items = gather_all(table.reshape(-1, LN), gram_part, 0)
        tables = tables.reshape(G, -1, F, LN)
        user_t, user_table, gram_part = half_step(8, True, 2, 6, tables, payload.reshape(G * PAY, LN),
                                                  gram_items, start_block.T)
        user_tables, gram_users = gather_all(user_table.reshape(-1, LN), gram_part, 1)
        user_tables = user_tables.reshape(G, -1, F, LN)
        item_new = half_step(2, False, 2, 8, user_tables, late.reshape(G * PAY, LN), gram_users, item_t)[0]
        return user_t.T, item_new.T

    return jax.shard_map(local_sweep, mesh=mesh,
                         in_specs=(part_spec, part_spec, slot_spec, slot_spec, slot_spec, slot_spec),
                         out_specs=(part_spec, part_spec), check_vma=False)
```

profile of v0, /device:TPU:1, one launch (start us, length us, event | category | flops | bytes accessed | tf_op | source)
XLA Modules:
  0.0 508.5 jit_solution(5493185628466276516)
XLA Ops:
  0.6 7.0 %user_payload.1 = f32[128,48,128]{2,1,0:T(8,128)} custom-call(s32[1]{0:T(128)} %bitcast.3.me_ref, s32[8,65536]{1,0:T(8,128)} %bitcast.30, f32[8,65536]{1,0:T(8,128)} %bitcast.31), custom_call_target="tpu_custom_call" | custom-call | tf_op jit(solution)/shard_map/user_payload/pallas_call | solution.py:100
  7.6 11.5 %all-to-all-start = ((f32[128,48,128]{2,1,0:T(8,128)}), f32[128,48,128]{2,1,0:T(8,128)S(1)}, u32[]{:S(2)}, u32[]{:S(2)}) async-start(f32[128,48,128]{2,1,0:T(8,128)} %user_payload.1), calls=%async_computation | async-start | bytes 6291456 | tf_op jit(solution)/shard_map/all_to_all | solution.py:558
  19.1 1.9 table.1
  21.1 127.3 %gather_all.2 = (bf16[4,4,4,2,1024,128]{5,4,3,2,1,0:T(8,128)(2,1)}, f32[4,4,4,2,32,128]{5,4,3,2,1,0:T(8,128)}) custom-call(bf16[1024,128]{1,0:T(8,128)(2,1)} %bitcast.36, f32[32,128]{1,0:T(8,128)} %get-tuple-element.12.refs_1_), custom_call_target="tpu_custom_call" | custom-call | tf_op jit(solution)/shard_map/gather_all/pallas_call | solution.py:257
  148.4 11.1 %item_payload.1 = f32[128,48,128]{2,1,0:T(8,128)} custom-call(s32[1]{0:T(128)} %bitcast.3.me_ref, s32[4096,128]{1,0:T(8,128)} %bitcast.32, f32[4096,128]{1,0:T(8,128)} %bitcast.33), custom_call_target="tpu_custom_call" | custom-call | tf_op jit(solution)/shard_map/item_payload/pallas_call | solution.py:139
  159.4 0.0 all-to-all-done
  159.4 0.0 copy-start
  159.4 1.6 copy-done
  161.1 5.4 %all-to-all-start.1 = ((f32[128,48,128]{2,1,0:T(8,128)}), f32[128,48,128]{2,1,0:T(8,128)}, u32[]{:S(2)}, u32[]{:S(2)}) async-start(f32[128,48,128]{2,1,0:T(8,128)} %item_payload.1), calls=%async_computation.1 | async-start | bytes 6291456 | tf_op jit(solution)/shard_map/all_to_all | solution.py:564
  166.5 173.8 %half_step.2 = (f32[64,512]{1,0:T(8,128)}, bf16[4,64,128]{2,1,0:T(8,128)(2,1)}, f32[32,128]{1,0:T(8,128)}) custom-call(bf16[128,16,64,128]{3,2,1,0:T(8,128)(2,1)} %bitcast.38, f32[6144,128]{1,0:T(8,128)} %bitcast.29, f32[4096,128]{1,0:T(8,128)} %bitcast.40, f32[64,512]{1,0:T(8,128)} %bitcast.42), custom_call_target="tpu_custom_call" | custom-call | flops 99999997952 | bytes 33554432 | tf_op jit(solution)/shard_map/half_step/pallas_call | solution.py:523
  340.3 52.3 %gather_all.3 = (bf16[4,4,4,2,256,128]{5,4,3,2,1,0:T(8,128)(2,1)}, f32[4,4,4,2,32,128]{5,4,3,2,1,0:T(8,128)}) custom-call(bf16[256,128]{1,0:T(8,128)(2,1)} %bitcast.37, f32[32,128]{1,0:T(8,128)} %get-tuple-element.17.refs_1_), custom_call_target="tpu_custom_call" | custom-call | tf_op jit(solution)/shard_map/gather_all/pallas_call | solution.py:257
  392.6 0.0 all-to-all-done.1
  392.6 115.9 %half_step.3 = f32[64,2048]{1,0:T(8,128)} custom-call(bf16[128,4,64,128]{3,2,1,0:T(8,128)(2,1)} %bitcast.39, f32[6144,128]{1,0:T(8,128)} %bitcast.20.pay_hbm, f32[4096,128]{1,0:T(8,128)} %bitcast.41, f32[64,2048]{1,0:T(8,128)} %bitcast.35), custom_call_target="tpu_custom_call" | custom-call | flops 99999997952 | bytes 33554432 | tf_op jit(solution)/shard_map/half_step/pallas_call | solution.py:523
Async XLA Ops:
  7.6 151.8 %all-to-all-start = ((f32[128,48,128]{2,1,0:T(8,128)}), f32[128,48,128]{2,1,0:T(8,128)S(1)}, u32[]{:S(2)}, u32[]{:S(2)}) async-start(f32[128,48,128]{2,1,0:T(8,128)} %user_payload.1), calls=%async_computation | async-start | bytes 6291456 | tf_op jit(solution)/shard_map/all_to_all | solution.py:558
  159.4 1.6 copy-start
  161.1 231.5 %all-to-all-start.1 = ((f32[128,48,128]{2,1,0:T(8,128)}), f32[128,48,128]{2,1,0:T(8,128)}, u32[]{:S(2)}, u32[]{:S(2)}) async-start(f32[128,48,128]{2,1,0:T(8,128)} %item_payload.1), calls=%async_computation.1 | async-start | bytes 6291456 | tf_op jit(solution)/shard_map/all_to_all | solution.py:564
where the time goes:
time: 509 us; the launch traced here: 508 us
  Pallas kernels  489 us (96%)
  starting transfers between devices  16.9 us (3%)
    pallas_call x2, Pallas kernels, half_step(): pl.pallas_call(functools.partial(half_kernel, slots, n // LN, pair, lanes...  290 us
    pallas_call x2, Pallas kernels, gather_all(): pl.pallas_call(functools.partial(gather_kernel, tuple(streams)), in_specs...  180 us
    all_to_all x1, starting transfers between devices, local_sweep(): payload = lax.all_to_all(payload, 'g', 0, 0, tiled=True)  11.5 us
    pallas_call x1, Pallas kernels, item_payload(): pl.pallas_call(item_payload_kernel, grid=(dests // step,), in_specs=[pl.B...  11.1 us
  transfers between devices with their start and end apart: 2, of which 0 were waited for; matrix products, arithmetic and copies ran while one was open for 0% of the time, Pallas kernels for 72%

commit v1 on v0

--- a/solution.py
+++ b/solution.py
@@ -107,8 +107,8 @@
     )(me, idx_t, conf_t)
 
 
-def item_payload_kernel(me_ref, idx_ref, conf_ref, out_ref):
-    skew = me_ref[0] % 64
+def arrange_items(me, idx_ref, conf_ref, out_ref):
+    skew = me % 64
     lane = iota((8, LN), 1)
     pattern = lane ^ skew
     low = lane < 64
@@ -133,28 +133,20 @@
     lax.fori_loop(0, out_ref.shape[0], place, 0, unroll=min(8, out_ref.shape[0]))
 
 
-def item_payload(me, idx_rows, conf_rows, dests):
-    step = min(32, dests)
-    spec = pl.BlockSpec((step * 32, LN), lambda i: (i, 0))
-    return pl.pallas_call(
-        item_payload_kernel,
-        grid=(dests // step,),
-        in_specs=[pl.BlockSpec(memory_space=pltpu.SMEM), spec, spec],
-        out_specs=pl.BlockSpec((step, PAY, LN), lambda i: (i, 0, 0)),
-        out_shape=jax.ShapeDtypeStruct((dests, PAY, LN), F32),
-        name='item_payload',
-    )(me, idx_rows, conf_rows)
-
-
 ORDERS = ((2, 1, 0), (1, 0, 2), (0, 2, 1))
 STRIDES = (32, 8, 2)
 RING = 4
 
 
-def gather_kernel(streams, *refs):
-    arrays = len({s[0] for s in streams})
-    ins, outs = refs[:arrays], refs[arrays:2 * arrays]
-    send, recv, pass_send, pass_recv, local = refs[2 * arrays:]
+def gather_kernel(streams, beside_work, *refs):
+    if beside_work:
+        table, gram, idx_hbm, conf_hbm, *outs, pay_hbm, send, recv, pass_send, pass_recv, local, idx, conf, pay, work = refs
+        loads = [pltpu.make_async_copy(idx_hbm, idx, work.at[0]), pltpu.make_async_copy(conf_hbm, conf, work.at[1])]
+        for copy in loads:
+            copy.start()
+    else:
+        table, gram, *outs, send, recv, pass_send, pass_recv, local = refs
+    ins = (table, gram)
     me = lax.axis_index('g')
     core = me % 2
     here = [me // stride % RING for stride in STRIDES]
@@ -195,6 +187,7 @@
         copy.start()
         passed.append(copy)
 
+    count = len(streams)
     own, kept = [], []
     for s, (which, first, rows, _) in enumerate(streams):
         src = ins[which].at[pl.ds(first, rows), :]
@@ -202,39 +195,58 @@
         copy = pltpu.make_async_copy(src, region(s, 0, 0, 0, None), local.at[s])
         copy.start()
         kept.append(copy)
-    sent = []
+    sent, across, further = [], {}, {}
+
+    def start_across(s, phase):
+        dim = ORDERS[streams[s][3]][phase]
+        for way, delta in enumerate((1, -1)):
+            mine = region(s, phase, dim, 0, None)
+            src = own[s] if phase == 0 else mine
+            across[s, way] = remote(src, mine, (send, recv), ((s * 3 + phase) * 2 + 0) * 2 + way, beside(dim, delta))
+            across[s, way].start()
+            sent.append(across[s, way])
+
+    def start_further(s, phase):
+        dim = ORDERS[streams[s][3]][phase]
+        for way, delta in enumerate((1, -1)):
+            across[s, way].wait_recv()
+            half = region(s, phase, dim, -delta, way)
+            further[s, way] = remote(half, half, (send, recv), ((s * 3 + phase) * 2 + 1) * 2 + way, beside(dim, delta))
+            further[s, way].start()
+            sent.append(further[s, way])
+        for way, delta in enumerate((1, -1)):
+            whole = region(s, phase, dim, -delta, None)
+            pass_on(whole, whole, s, 1 + 4 * phase + way)
+
+    def finish(s, phase):
+        dim = ORDERS[streams[s][3]][phase]
+        for way in range(2):
+            further[s, way].wait_recv()
+        if phase == 0:
+            kept[s].wait()
+        if phase < 2:
+            start_across(s, phase + 1)
+        for way in range(2):
+            half = region(s, phase, dim, 2, way)
+            pass_on(half, half, s, 3 + 4 * phase + way)
+
+    for s in range(count):
+        start_across(s, 0)
+    for s in range(count):
+        pass_on(own[s], region(s, 0, 0, 0, None), s, 0)
     for phase in range(3):
-        across = {}
-        for s in range(len(streams)):
-            dim = ORDERS[streams[s][3]][phase]
-            for way, delta in enumerate((1, -1)):
-                mine = region(s, phase, dim, 0, None)
-                src = own[s] if phase == 0 else mine
-                across[s, way] = remote(src, mine, (send, recv), ((s * 3 + phase) * 2 + 0) * 2 + way, beside(dim, delta))
-                across[s, way].start()
-        if phase == 0:
-            for s in range(len(streams)):
-                pass_on(own[s], region(s, 0, 0, 0, None), s, 0)
-        further = {}
-        for s in range(len(streams)):
-            dim = ORDERS[streams[s][3]][phase]
-            for way, delta in enumerate((1, -1)):
-                across[s, way].wait_recv()
-                half = region(s, phase, dim, -delta, way)
-                further[s, way] = remote(half, half, (send, recv), ((s * 3 + phase) * 2 + 1) * 2 + way, beside(dim, delta))
-                further[s, way].start()
-                whole = region(s, phase, dim, -delta, None)
-                pass_on(whole, whole, s, 1 + 4 * phase + way)
-        for s in range(len(streams)):
-            dim = ORDERS[streams[s][3]][phase]
-            for way in range(2):
-                further[s, way].wait_recv()
-                half = region(s, phase, dim, 2, way)
-                pass_on(half, half, s, 3 + 4 * phase + way)
-        if phase == 0:
-            for copy in kept:
+        for s in range(count):
+            start_further(s, phase)
+        for s in range(count):
+            finish(s, phase)
+        if phase == 1 and beside_work:
+            for copy in loads:
                 copy.wait()
-        sent += list(across.values()) + list(further.values())
+            arrange_items(me, idx, conf, pay)
+            store = pltpu.make_async_copy(pay, pay_hbm, work.at[2])
+            store.start()
+    if beside_work:
+        store.wait()
     for copy in sent:
         copy.wait_send()
     for copy in passed:
@@ -243,29 +255,36 @@
         copy.wait_recv()
 
 
-def gather_all(table, gram, collective_id):
+def gather_all(table, gram, collective_id, slot_rows=()):
     rows = table.shape[0]
-    third = rows // 3 // 32 * 32
-    sizes = (rows - 2 * third, third, third)
-    streams, first = [], 0
+    units = rows // 16
+    large = -(-units // 6)
+    sizes = (large, large, (units - 4 * large) // 2) * 2
+    streams, first = [(1, 0, gram.shape[0], 2)], 0
     for n, size in enumerate(sizes):
-        streams.append((0, first, size, n))
-        first += size
-    streams.append((1, 0, gram.shape[0], 0))
+        streams.append((0, first, 16 * size, n % 3))
+        first += 16 * size
     count = len(streams)
     any_spec = pl.BlockSpec(memory_space=pl.ANY)
-    tables, grams = pl.pallas_call(
-        functools.partial(gather_kernel, tuple(streams)),
-        in_specs=[pl.BlockSpec(memory_space=pltpu.VMEM)] * 2,
-        out_specs=[any_spec] * 2,
-        out_shape=[jax.ShapeDtypeStruct((RING, RING, RING, 2, *x.shape), x.dtype) for x in (table, gram)],
-        scratch_shapes=[pltpu.SemaphoreType.DMA((12 * count,)), pltpu.SemaphoreType.DMA((12 * count,)),
-                        pltpu.SemaphoreType.DMA((13 * count,)), pltpu.SemaphoreType.DMA((13 * count,)),
-                        pltpu.SemaphoreType.DMA((count,))],
+    out_shape = [jax.ShapeDtypeStruct((RING, RING, RING, 2, *x.shape), x.dtype) for x in (table, gram)]
+    scratch = [pltpu.SemaphoreType.DMA((12 * count,)), pltpu.SemaphoreType.DMA((12 * count,)),
+               pltpu.SemaphoreType.DMA((13 * count,)), pltpu.SemaphoreType.DMA((13 * count,)),
+               pltpu.SemaphoreType.DMA((count,))]
+    if slot_rows:
+        dests = slot_rows[0].shape[0] // 32
+        out_shape.append(jax.ShapeDtypeStruct((dests, PAY, LN), F32))
+        scratch += [pltpu.VMEM(x.shape, x.dtype) for x in slot_rows]
+        scratch += [pltpu.VMEM((dests, PAY, LN), F32), pltpu.SemaphoreType.DMA((3,))]
+    tables, grams, *payload = pl.pallas_call(
+        functools.partial(gather_kernel, tuple(streams), bool(slot_rows)),
+        in_specs=[pl.BlockSpec(memory_space=pltpu.VMEM)] * 2 + [any_spec] * len(slot_rows),
+        out_specs=[any_spec] * len(out_shape),
+        out_shape=out_shape,
+        scratch_shapes=scratch,
         compiler_params=pltpu.CompilerParams(collective_id=collective_id, has_side_effects=True),
         name='gather_all',
-    )(table, gram)
-    return tables.reshape(G, rows, LN), grams.reshape(-1, LN)
+    )(table, gram, *slot_rows)
+    return tables.reshape(G, rows, LN), grams.reshape(-1, LN), *payload
 
 
 def half_kernel(slots, blocks, pair, lanes_of, emit, tab_hbm, pay_hbm, gram_ref, x0_ref, *refs):
@@ -560,11 +579,9 @@
         def as_rows(x):
             return x[0].reshape(-1, LN, 2).transpose(0, 2, 1).reshape(-1, LN)
 
-        late = item_payload(me, as_rows(user_idx), as_rows(user_conf), G)
+        tables, gram_items, late = gather_all(table.reshape(-1, LN), gram_part, 0, (as_rows(user_idx), as_rows(user_conf)))
+        tables = tables.reshape(G, -1, F, LN)
         late = lax.all_to_all(late, 'g', 0, 0, tiled=True)
-
-        tables, gram_items = gather_all(table.reshape(-1, LN), gram_part, 0)
-        tables = tables.reshape(G, -1, F, LN)
         user_t, user_table, gram_part = half_step(8, True, 2, 6, tables, payload.reshape(G * PAY, LN),
                                                   gram_items, start_block.T)
         user_tables, gram_users = gather_all(user_table.reshape(-1, LN), gram_part, 1)

time: 509 us -> 473 us (0.929)
  Pallas kernels: 489 us -> 453 us
    pallas_call x3 -> x2, Pallas kernels: 191 us -> 154 us  [gather_all(): pl.pallas_call(functools.partial(gather_kernel, tuple(streams), bool(slot...]
  transfers between devices with their start and end apart: 2 -> 2, of which waited for: 0 -> 0; matrix products, arithmetic and copies ran while one was open for 0% -> 0% of each run, Pallas kernels for 72% -> 70%
where the time goes in v1:
time: 473 us
  Pallas kernels  453 us (96%)
  starting transfers between devices  17.4 us (4%)
    pallas_call x2, Pallas kernels, half_step(): pl.pallas_call(functools.partial(half_kernel, slots, n // LN, pair, lanes...  290 us
    pallas_call x2, Pallas kernels, gather_all(): pl.pallas_call(functools.partial(gather_kernel, tuple(streams), bool(slot...  154 us
    all_to_all x1, starting transfers between devices, local_sweep(): payload = lax.all_to_all(payload, 'g', 0, 0, tiled=True)  11.5 us
  transfers between devices with their start and end apart: 2, of which 0 were waited for; matrix products, arithmetic and copies ran while one was open for 0% of the time, Pallas kernels for 70%

profile of v1, /device:TPU:1, one launch (start us, length us, event | category | flops | bytes accessed | tf_op | source)
XLA Modules:
  0.0 472.5 jit_solution(3343077392746386226)
XLA Ops:
  0.6 7.0 %user_payload.1 = f32[128,48,128]{2,1,0:T(8,128)} custom-call(s32[1]{0:T(128)} %bitcast.9.me_ref, s32[8,65536]{1,0:T(8,128)} %bitcast.32, f32[8,65536]{1,0:T(8,128)} %bitcast.33), custom_call_target="tpu_custom_call" | custom-call | tf_op jit(solution)/shard_map/user_payload/pallas_call | solution.py:100
  7.6 11.5 %all-to-all-start = ((f32[128,48,128]{2,1,0:T(8,128)}), f32[128,48,128]{2,1,0:T(8,128)S(1)}, u32[]{:S(2)}, u32[]{:S(2)}) async-start(f32[128,48,128]{2,1,0:T(8,128)} %user_payload.1), calls=%async_computation | async-start | bytes 6291456 | tf_op jit(solution)/shard_map/all_to_all | solution.py:577
  19.1 1.9 table.1
  21.1 110.9 %gather_all.2 = (bf16[4,4,4,2,1024,128]{5,4,3,2,1,0:T(8,128)(2,1)}, f32[4,4,4,2,32,128]{5,4,3,2,1,0:T(8,128)}, f32[128,48,128]{2,1,0:T(8,128)}) custom-call(bf16[1024,128]{1,0:T(8,128)(2,1)} %bitcast.36, f32[32,128]{1,0:T(8,128)} %get-tuple-element.13.refs_1_, s32[4096,128]{1,0:T(8,128)} %bitcast.30, f32[4096,128]{1,0:T(8,128)} %bitcast.31), custom_call_target="tpu_custom_call" | custom-call | tf_op jit(solution)/shard_map/gather_all/pallas_call | solution.py:278
  132.0 0.0 all-to-all-done
  132.0 0.0 copy-start
  132.0 1.6 copy-done
  133.6 5.9 %all-to-all-start.1 = ((f32[128,48,128]{2,1,0:T(8,128)}), f32[128,48,128]{2,1,0:T(8,128)}, u32[]{:S(2)}, u32[]{:S(2)}) async-start(f32[128,48,128]{2,1,0:T(8,128)} %get-tuple-element.20), calls=%async_computation.1 | async-start | bytes 6291456 | tf_op jit(solution)/shard_map/all_to_all | solution.py:584
  139.6 173.8 %half_step.2 = (f32[64,512]{1,0:T(8,128)}, bf16[4,64,128]{2,1,0:T(8,128)(2,1)}, f32[32,128]{1,0:T(8,128)}) custom-call(bf16[128,16,64,128]{3,2,1,0:T(8,128)(2,1)} %bitcast.38, f32[6144,128]{1,0:T(8,128)} %bitcast.29, f32[4096,128]{1,0:T(8,128)} %bitcast.40, f32[64,512]{1,0:T(8,128)} %bitcast.42), custom_call_target="tpu_custom_call" | custom-call | flops 99999997952 | bytes 33554432 | tf_op jit(solution)/shard_map/half_step/pallas_call | solution.py:542
  313.4 43.2 %gather_all.3 = (bf16[4,4,4,2,256,128]{5,4,3,2,1,0:T(8,128)(2,1)}, f32[4,4,4,2,32,128]{5,4,3,2,1,0:T(8,128)}) custom-call(bf16[256,128]{1,0:T(8,128)(2,1)} %bitcast.37, f32[32,128]{1,0:T(8,128)} %get-tuple-element.18.refs_1_), custom_call_target="tpu_custom_call" | custom-call | tf_op jit(solution)/shard_map/gather_all/pallas_call | solution.py:278
  356.7 0.0 all-to-all-done.1
  356.7 115.9 %half_step.3 = f32[64,2048]{1,0:T(8,128)} custom-call(bf16[128,4,64,128]{3,2,1,0:T(8,128)(2,1)} %bitcast.39, f32[6144,128]{1,0:T(8,128)} %bitcast.20.pay_hbm, f32[4096,128]{1,0:T(8,128)} %bitcast.41, f32[64,2048]{1,0:T(8,128)} %bitcast.35), custom_call_target="tpu_custom_call" | custom-call | flops 99999997952 | bytes 33554432 | tf_op jit(solution)/shard_map/half_step/pallas_call | solution.py:542
Async XLA Ops:
  7.6 124.3 %all-to-all-start = ((f32[128,48,128]{2,1,0:T(8,128)}), f32[128,48,128]{2,1,0:T(8,128)S(1)}, u32[]{:S(2)}, u32[]{:S(2)}) async-start(f32[128,48,128]{2,1,0:T(8,128)} %user_payload.1), calls=%async_computation | async-start | bytes 6291456 | tf_op jit(solution)/shard_map/all_to_all | solution.py:577
  132.0 1.6 copy-start
  133.6 223.0 %all-to-all-start.1 = ((f32[128,48,128]{2,1,0:T(8,128)}), f32[128,48,128]{2,1,0:T(8,128)}, u32[]{:S(2)}, u32[]{:S(2)}) async-start(f32[128,48,128]{2,1,0:T(8,128)} %get-tuple-element.20), calls=%async_computation.1 | async-start | bytes 6291456 | tf_op jit(solution)/shard_map/all_to_all | solution.py:584
